TPU v7x, 256 devices: a whole 4x4x8 slice. The times are simulated.
256 devices in a mesh: member: 2 (over y_hi), seq: 32 (over z, x), head: 4 (over y_lo, core).
Axes of the slice: x: 4, y: 4 (y_hi: 2, y_lo: 2; y = y_hi * 2 + y_lo), z: 8, core: 2. Of those that a mesh axis runs over, the one named last changes fastest.
Arguments:
- tokens: bfloat16 [16384, 5120], P(('seq', 'head')), may hold values from -24 to 24
- lattice: int32 [3, 16384], P(None, 'seq'), may hold values from 0 to 63
- timestep: int32 [32], replicated, may hold values from 0 to 999
- time_weight: bfloat16 [2, 256, 5120], P(None, None, 'seq'), may hold values from -0.375 to 0.375
- query_weight: bfloat16 [2, 5120, 2560], P('member', 'seq', 'head'), may hold values from -6 to 6
- key_weight: bfloat16 [5120, 2560], P('seq', 'head'), may hold values from -6 to 6
- values: bfloat16 [16384, 2560], P(('seq', 'head')), may hold values from -6 to 6
- cotangent: bfloat16 [2, 16384, 2560], P('member', ('seq', 'head')), may hold values from -72 to 72
Outputs:
- fisher: float32 [2, 5120, 2560], P('member', 'seq', 'head')
- merged: float32 [5120, 2560], P('seq', 'head')
All inputs are finite; a program needn't handle non-finite values.
Results may differ from a plain program's by a relative error of at most 0.022.
Values may be sent and summed in bfloat16 or wider, within the bound.
A program may use at most 128 MiB of HBM per device.

v0:
```python
import math
import jax
import jax.numpy as jnp
from jax import lax
from jax.sharding import Mesh
from jax.sharding import PartitionSpec as P

HEAD_SIZE = 128
SEQ = ("seq_0", "seq_1")
SEQ_HEAD = ("seq_0", "seq_1", "head")
damping = 0.01


def side_by_side(arrays, axis, dim, along):
    widths = [a.shape[along] for a in arrays]
    both = jnp.concatenate(arrays, axis=along)
    out = lax.all_gather(both, axis, axis=dim, tiled=True)
    return tuple(jnp.split(out, [sum(widths[:k]) for k in range(1, len(widths))], axis=along))


def own_rows(terms, axes):
    subtotal = terms.astype(jnp.bfloat16)
    for axis in axes:
        subtotal = lax.psum_scatter(subtotal, axis, scatter_dimension=0, tiled=True)
    return subtotal.astype(jnp.float32)


def copy_for_each(array, axis):
    size = lax.axis_size(axis)
    return lax.all_to_all(
        jnp.broadcast_to(array[None], (size, *array.shape)), axis, 0, 0, tiled=True
    )


def of_everyone(array, axis):
    everything = copy_for_each(array, axis)
    return jnp.sum(everything.astype(jnp.float32), axis=0)


def time_features(timestep, feature_count):
    halfway = feature_count // 2
    ladder = jnp.arange(halfway).astype(jnp.float32)
    frequency = jnp.exp(-math.log(10000.0) * 2.0 * ladder / feature_count)
    angles = timestep.astype(jnp.float32)[:, None] * frequency[None, :]
    return jnp.concatenate([jnp.cos(angles), jnp.sin(angles)], axis=1).astype(jnp.bfloat16)


def rope_tables(lattice, head_width):
    halfway = head_width // 2
    side_pairs = head_width // 6
    frame_pairs = halfway - 2 * side_pairs
    column = jnp.arange(head_width)
    pair_index = column % halfway
    which_axis = jnp.where(
        pair_index < frame_pairs, 0, jnp.where(pair_index < frame_pairs + side_pairs, 1, 2)
    )
    anchor = jnp.where(
        which_axis == 0, 0, jnp.where(which_axis == 1, frame_pairs, frame_pairs + side_pairs)
    )
    pair_span = jnp.where(which_axis == 0, frame_pairs, side_pairs)
    frequency = jnp.exp(
        -math.log(10000.0)
        * (pair_index - anchor).astype(jnp.float32)
        / pair_span.astype(jnp.float32)
    )
    position = lattice.astype(jnp.float32)
    angles = jnp.zeros((lattice.shape[1], head_width), jnp.float32)
    for axis_number in range(3):
        chosen = jnp.where(which_axis == axis_number, frequency, 0.0)
        angles = angles + position[axis_number][:, None] * chosen[None, :]
    sign_flip = jnp.where(column < halfway, -1.0, 1.0).astype(jnp.float32)
    return (jnp.cos(angles), jnp.sin(angles) * sign_flip[None, :])


def normed_rotation(stacked, cosine, sine_table):
    halfway = stacked.shape[2] // 2
    inverse = lax.rsqrt(jnp.mean(stacked * stacked, axis=2, keepdims=True) + 1e-06)
    normed = stacked * inverse
    rotated = (
        normed * cosine[:, None, :] + jnp.roll(normed, halfway, axis=2) * sine_table[:, None, :]
    )
    return (normed, inverse, rotated)


def attention_backward(query_pre, key_pre, values, cotangent, cosine, sine_table, head_width):
    length, width = query_pre.shape
    head_count = width // head_width
    halfway = head_width // 2
    query_normed, query_inverse, query_rotated = normed_rotation(
        query_pre.reshape(length, head_count, head_width), cosine, sine_table
    )
    unused_normed, unused_inverse, key_rotated = normed_rotation(
        key_pre.reshape(length, head_count, head_width), cosine, sine_table
    )
    query_round = query_rotated.astype(jnp.bfloat16)
    key_round = key_rotated.astype(jnp.bfloat16)
    value_heads = values.reshape(length, head_count, head_width)
    block_rows = min(length, 512)
    block_count = length // block_rows
    score_scale = head_width ** (-0.5)

    def one_block(portion):
        query_block, grad_block = portion
        scores = (
            jnp.einsum("qhd,khd->hqk", query_block, key_round, preferred_element_type=jnp.float32)
            * score_scale
        )
        raised = jnp.exp(scores)
        weights = raised / jnp.sum(raised, axis=2, keepdims=True)
        rounded = weights.astype(jnp.bfloat16)
        attended = jnp.einsum(
            "hqk,khd->qhd", rounded, value_heads, preferred_element_type=jnp.float32
        )
        inner = jnp.sum(grad_block.astype(jnp.float32) * attended, axis=2)
        grad_weights = jnp.einsum(
            "qhd,khd->hqk", grad_block, value_heads, preferred_element_type=jnp.float32
        )
        grad_scores = (weights * (grad_weights - inner.T[:, :, None])).astype(jnp.bfloat16)
        return (
            jnp.einsum("hqk,khd->qhd", grad_scores, key_round, preferred_element_type=jnp.float32)
            * score_scale
        )

    grad_rotated = lax.map(
        one_block,
        (
            query_round.reshape(block_count, block_rows, head_count, head_width),
            cotangent.reshape(block_count, block_rows, head_count, head_width),
        ),
    )
    grad_rotated = grad_rotated.reshape(length, head_count, head_width)
    grad_normed = grad_rotated * cosine[:, None, :] + jnp.roll(
        grad_rotated * sine_table[:, None, :], halfway, axis=2
    )
    grad_query = query_inverse * (
        grad_normed - query_normed * jnp.mean(grad_normed * query_normed, axis=2, keepdims=True)
    )
    return grad_query.reshape(length, width).astype(jnp.bfloat16)


def on_device(tokens, lattice, timestep, time_weight, query_weight, key_weight, values, cotangent):
    features = time_features(timestep, time_weight.shape[1])
    local_shift = jnp.einsum(
        "cf,jfd->cjd", features, time_weight, preferred_element_type=jnp.float32
    )
    own_shift = lax.all_to_all(
        local_shift.astype(jnp.bfloat16), SEQ, split_axis=0, concat_axis=2, tiled=True
    ).astype(local_shift.dtype)
    hidden = tokens.astype(jnp.float32)
    average = jnp.mean(hidden, axis=1, keepdims=True)
    centred = hidden - average
    variance = jnp.mean(centred * centred, axis=1, keepdims=True)
    normed = centred * lax.rsqrt(variance + 1e-06)
    modulated = (normed * (1.0 + own_shift[0, 1][None, :]) + own_shift[0, 0][None, :]).astype(
        jnp.bfloat16
    )
    clip_rows = lax.all_gather(modulated, "head", axis=0, tiled=True)
    cosine, sine_table = rope_tables(lattice, HEAD_SIZE)
    own_query = query_weight[0]

    def contract(portion):
        return jnp.dot(clip_rows, portion, preferred_element_type=jnp.float32)

    portions = side_by_side((own_query, key_weight), SEQ, 0, 1)
    query_pre = contract(portions[0])
    key_pre = contract(portions[1])
    value_heads, cot_heads = (
        lax.all_to_all(values, "head", split_axis=1, concat_axis=0, tiled=True),
        lax.all_to_all(cotangent[0], "head", split_axis=1, concat_axis=0, tiled=True),
    )
    grad_query = attention_backward(
        query_pre, key_pre, value_heads, cot_heads, cosine, sine_table, HEAD_SIZE
    )
    grad = lax.dot_general(
        clip_rows, grad_query, (((0,), (0,)), ((), ())), preferred_element_type=jnp.float32
    )
    fisher = own_rows(grad * grad, SEQ)
    weighted = fisher + damping
    upper = weighted * own_query.astype(jnp.float32)
    upper_sum, lower_sum = (
        of_everyone(upper.astype(jnp.bfloat16), "member").astype(jnp.float32),
        of_everyone(weighted.astype(jnp.bfloat16), "member").astype(jnp.float32),
    )
    merged = upper_sum / lower_sum
    return (fisher[None], merged)


def solution(mesh):
    finer = Mesh(
        mesh.devices.reshape(mesh.shape["member"], 8, 4, mesh.shape["head"]),
        ("member", "seq_0", "seq_1", "head"),
    )
    in_specs = (
        P(SEQ_HEAD, None),
        P(None, SEQ),
        P(),
        P(None, None, SEQ),
        P("member", SEQ, "head"),
        P(SEQ, "head"),
        P(SEQ_HEAD, None),
        P("member", SEQ_HEAD, None),
    )
    out_specs = (P("member", SEQ, "head"), P(SEQ, "head"))
    return jax.shard_map(
        on_device, mesh=finer, in_specs=in_specs, out_specs=out_specs, check_vma=False
    )
```

profile of v0, /device:TPU:32, one launch (start us, length us, event | category | flops | bytes accessed | tf_op | source)
XLA Modules:
  0.0 387.7 jit_solution(6202035833007734098)
XLA Ops:
  7.2 0.8 convert_element_type.123
  8.0 0.1 fusion.42
  8.1 0.1 convolution_convert_fusion
  8.3 0.7 copy.51
  8.9 11.2 %all-to-all-start = ((bf16[32,2,160]{2,1,0:T(2,128)(2,1)}), bf16[32,2,160]{2,1,0:T(2,128)(2,1)S(1)}, u32[]{:S(2)}, u32[]{:S(2)}) async-start(bf16[32,2,160]{2,1,0:T(2,128)(2,1)} %copy.51), calls=%async_computation | async-start | bytes 65536 | tf_op jit(solution)/shard_map/all_to_all | solution.py:146
  20.1 0.0 all-gather.3.cloned.1.call-start
  20.2 1.6 convert_reduce_fusion
  21.8 0.5 fusion.8
  22.3 6.5 %all-to-all-done = bf16[32,2,160]{2,1,0:T(2,128)(2,1)S(1)} async-done(((bf16[32,2,160]{2,1,0:T(2,128)(2,1)}), bf16[32,2,160]{2,1,0:T(2,128)(2,1)S(1)}, u32[]{:S(2)}, u32[]{:S(2)}) %all-to-all-start) | async-done | bytes 20512 | tf_op jit(solution)/shard_map/all_to_all | solution.py:146
  28.9 0.1 reshape.306
  29.0 1.7 fusion.11
  30.7 0.0 all-gather.3.cloned.1.call-update
  30.7 0.0 all-gather.5.cloned.1.call-start
  30.8 0.9 copy-done.6
  31.6 0.1 copy-done.13
  31.7 0.8 pad_maximum_fusion
  32.5 1.1 copy.59
  33.6 3.5 all-to-all-start.2
  37.2 1.1 copy.57
  38.2 14.3 %all-to-all-done.2 = bf16[128,4,640]{0,2,1:T(8,128)(2,1)S(1)} async-done(((bf16[128,4,640]{0,2,1:T(8,128)(2,1)}), bf16[128,4,640]{0,2,1:T(8,128)(2,1)S(1)}, u32[]{:S(2)}, u32[]{:S(2)}) %all-to-all-start.2) | async-done | bytes 655392 | tf_op jit(solution)/shard_map/all_to_all | solution.py:168
  52.5 3.5 all-to-all-start.1
  56.0 0.0 reduce-scatter.3.cloned.1.call-start
  56.1 2.0 broadcast_multiply_fusion.3
  58.1 0.5 copy.60
  58.6 1.1 reshape.305
  59.8 13.9 %all-to-all-done.1 = bf16[128,4,640]{0,2,1:T(8,128)(2,1)S(1)} async-done(((bf16[128,4,640]{0,2,1:T(8,128)(2,1)}), bf16[128,4,640]{0,2,1:T(8,128)(2,1)S(1)}, u32[]{:S(2)}, u32[]{:S(2)}) %all-to-all-start.1) | async-done | bytes 655392 | tf_op jit(solution)/shard_map/all_to_all | solution.py:169
  73.6 0.5 copy.58
  74.2 1.1 squeeze.12
  75.2 21.1 %all-gather.3.cloned.1.call-done = bf16[512,5120]{1,0:T(8,128)(2,1)} async-done(((bf16[128,5120]{1,0:T(8,128)(2,1)}), bf16[512,5120]{1,0:T(8,128)(2,1)}) %all-gather.3.cloned.1.call-update) | async-done | bytes 5242896 | tf_op jit(solution)/shard_map/all_gather | solution.py:157
  96.3 118.9 %all-gather.5.cloned.1.call-done = bf16[5120,1280]{1,0:T(8,128)(2,1)} async-done(((bf16[160,1280]{1,0:T(8,128)(2,1)}), bf16[5120,1280]{1,0:T(8,128)(2,1)}) %all-gather.5.cloned.1.call-update) | async-done | bytes 13107216 | tf_op jit(solution)/shard_map/all_gather | solution.py:17
  215.2 8.4 %fusion = f32[512,640]{0,1:T(8,128)S(1)} fusion(bf16[512,5120]{1,0:T(8,128)(2,1)} %all-gather.3.cloned.1.call-done, bf16[5120,1280]{1,0:T(8,128)(2,1)} %all-gather.5.cloned.1.call-done), kind=kOutput, calls=%fused_computation.1 | convolution fusion | flops 3355443200 | bytes 13107200 | tf_op jit(solution)/shard_map/dot_general | solution.py:162
  223.6 0.2 multiply_reduce_fusion.1
  223.8 0.1 broadcast_multiply_fusion.1
  223.9 0.1 fusion.55
  224.0 2.2 copy-done.15
  226.3 6.0 %fusion.2 = f32[512,640]{0,1:T(8,128)S(1)} fusion(bf16[512,5120]{1,0:T(8,128)(2,1)S(1)} %copy-done.15, bf16[5120,1280]{1,0:T(8,128)(2,1)} %all-gather.5.cloned.1.call-done), kind=kOutput, calls=%fused_computation.3 | convolution fusion | flops 3355443200 | bytes 13107200 | tf_op jit(solution)/shard_map/dot_general | solution.py:162
  232.2 0.2 multiply_reduce_fusion.2
  232.4 0.1 broadcast_multiply_fusion.2
  232.6 0.1 fusion.54
  232.7 0.8 copy-done.4
  233.5 0.1 copy-done.5
  233.6 0.4 fusion.28
  234.0 1.2 fusion.5
  235.3 1.2 fusion.31
  236.5 1.1 copy-done.2
  237.6 5.9 %broadcast_multiply_fusion = (f32[512,5,128]{0,2,1:T(8,128)}, f32[512,5,128]{0,2,1:T(8,128)S(1)}) fusion(f32[512,128]{0,1:T(8,128)} %get-tuple-element.30, bf16[512,5,128]{0,2,1:T(8,128)(2,1)S(1)} %fusion.28, bf16[512,5,128]{0,2,1:T(8,128)(2,1)} %squeeze.12, bf16[512,5,128]{0,2,1:T(8,128)(2,1)} %reshape.305, f32[5,512]{1,0:T(8,128)S(1)} %bitcast.67, ...), kind=kOutput, calls=%fused_computation.41 | convolution fusion | flops 677969920 | bytes 10113024 | tf_op jit(solution)/shard_map/while/body/eval_jaxpr/hqk,khd->qhd/dot_general | solution.py:120
  243.5 1.6 fusion.53
  245.1 0.5 multiply_reduce_fusion
  245.6 0.6 multiply_convert_fusion.5
  246.2 0.4 slice-done.1
  246.7 6.3 %multiply_convert_fusion = bf16[5120,640]{1,0:T(8,128)(2,1)} fusion(bf16[512,5120]{1,0:T(8,128)(2,1)S(1)} %bitcast.66, bf16[512,640]{0,1:T(8,128)(2,1)S(1)} %bitcast.59), kind=kOutput, calls=%fused_computation | convolution fusion | flops 3361996800 | bytes 12451840 | tf_op jit(solution)/shard_map/dot_general | solution.py:174
  252.9 0.0 reduce-scatter.3.cloned.1.call-update
  252.9 0.0 reduce-scatter.5.cloned.1.call-start
  253.0 74.8 %reduce-scatter.3.cloned.1.call-done = bf16[640,640]{1,0:T(8,128)(2,1)} async-done(((bf16[5120,640]{1,0:T(8,128)(2,1)}), bf16[640,640]{1,0:T(8,128)(2,1)}) %reduce-scatter.3.cloned.1.call-update) | async-done | bytes 819216 | tf_op jit(solution)/shard_map/reduce_scatter | solution.py:24
  327.8 27.9 %reduce-scatter.5.cloned.1.call-done = bf16[160,640]{1,0:T(8,128)(2,1)} async-done(((bf16[640,640]{1,0:T(8,128)(2,1)}), bf16[160,640]{1,0:T(8,128)(2,1)}) %reduce-scatter.5.cloned.1.call-update) | async-done | bytes 204816 | tf_op jit(solution)/shard_map/reduce_scatter | solution.py:24
  355.8 1.0 fusion.38
  356.8 11.7 %all_to_all.51 = bf16[2,160,640]{2,1,0:T(8,128)(2,1)S(1)} all-to-all(bf16[2,160,640]{2,1,0:T(8,128)(2,1)S(1)} %broadcast_in_dim.82), channel_id=1, replica_groups=mesh['member'=2,'seq_0'=8,'seq_1'=4,'head'=4] {'member'}, dimensions={0} | all-to-all | bytes 819200 | tf_op jit(solution)/shard_map/all_to_all | solution.py:30
  368.6 0.8 broadcast_in_dim.81
  369.3 3.5 all-to-all-start.3
  372.8 0.8 convert_bitcast_fusion
  373.6 0.1 convert_reduce_fusion.1
  373.7 6.6 %all-to-all-done.3 = bf16[2,160,640]{2,1,0:T(8,128)(2,1)S(1)} async-done(((bf16[2,160,640]{2,1,0:T(8,128)(2,1)}), bf16[2,160,640]{2,1,0:T(8,128)(2,1)S(1)}, u32[]{:S(2)}, u32[]{:S(2)}) %all-to-all-start.3) | async-done | bytes 409632 | tf_op jit(solution)/shard_map/all_to_all | solution.py:30
  380.3 0.1 convert_reduce_fusion.2
  380.3 0.9 div.63
  (46 shorter events, 0.3 us)
Async XLA Ops:
  7.2 1.0 copy-start
  7.2 14.6 %copy-start.1 = (bf16[128,5120]{1,0:T(8,128)(2,1)S(1)}, bf16[128,5120]{1,0:T(8,128)(2,1)}, u32[]{:S(2)}) copy-start(bf16[128,5120]{1,0:T(8,128)(2,1)} %param.8) | copy-start | bytes 3932164
  8.9 19.9 %all-to-all-start = ((bf16[32,2,160]{2,1,0:T(2,128)(2,1)}), bf16[32,2,160]{2,1,0:T(2,128)(2,1)S(1)}, u32[]{:S(2)}, u32[]{:S(2)}) async-start(bf16[32,2,160]{2,1,0:T(2,128)(2,1)} %copy.51), calls=%async_computation | async-start | bytes 65536 | tf_op jit(solution)/shard_map/all_to_all | solution.py:146
  20.1 76.2 %all-gather.3.cloned.1.call-start = ((), (), s32[]{:S(2)}) async-start(), calls=%async_computation.7 | async-start | bytes 6553600 | tf_op jit(solution)/shard_map/all_gather | solution.py:157
  30.7 0.9 copy-start.6
  30.7 1.0 copy-start.13
  30.7 1.8 copy-start.9
  30.7 184.5 %all-gather.5.cloned.1.call-start = ((), (), s32[]{:S(2)}) async-start(), calls=%async_computation.8 | async-start | bytes 13516800 | tf_op jit(solution)/shard_map/all_gather | solution.py:17
  32.5 4.6 %copy-start.10 = (bf16[1,128,2560]{2,1,0:T(8,128)(2,1)S(1)}, bf16[1,128,2560]{2,1,0:T(8,128)(2,1)}, u32[]{:S(2)}) copy-start(bf16[1,128,2560]{2,1,0:T(8,128)(2,1)} %param.15) | copy-start | bytes 1966084
  33.6 18.9 %all-to-all-start.2 = ((bf16[128,4,640]{0,2,1:T(8,128)(2,1)}), bf16[128,4,640]{0,2,1:T(8,128)(2,1)S(1)}, u32[]{:S(2)}, u32[]{:S(2)}) async-start(bf16[128,4,640]{0,2,1:T(8,128)(2,1)} %bitcast.13), calls=%async_computation.2 | async-start | bytes 1310720 | tf_op jit(solution)/shard_map/all_to_all | solution.py:168
  37.1 18.9 %copy-start.14 = (s32[3,512]{1,0:T(4,128)S(1)}, s32[3,512]{1,0:T(4,128)}, u32[]{:S(2)}) copy-start(s32[3,512]{1,0:T(4,128)} %param.9) | copy-start | bytes 18436
  52.5 21.1 %all-to-all-start.1 = ((bf16[128,4,640]{0,2,1:T(8,128)(2,1)}), bf16[128,4,640]{0,2,1:T(8,128)(2,1)S(1)}, u32[]{:S(2)}, u32[]{:S(2)}) async-start(bf16[128,4,640]{0,2,1:T(8,128)(2,1)} %bitcast.11), calls=%async_computation.1 | async-start | bytes 1310720 | tf_op jit(solution)/shard_map/all_to_all | solution.py:169
  56.0 271.8 %reduce-scatter.3.cloned.1.call-start = ((), (), s32[]{:S(2)}) async-start(), calls=%async_computation.9 | async-start | bytes 7372800 | tf_op jit(solution)/shard_map/reduce_scatter | solution.py:24
  223.8 2.5 copy-start.15
  232.6 1.0 copy-start.4
  232.6 1.0 copy-start.5
  234.0 1.3 copy-start.11
  234.0 1.3 copy-start.12
  235.3 2.3 copy-start.2
  243.5 1.6 copy-start.3
  243.5 2.7 slice-start
  245.1 1.6 slice-start.1
  252.9 102.9 %copy-start.7 = (bf16[1,160,640]{2,1,0:T(8,128)(2,1)S(1)}, bf16[1,160,640]{2,1,0:T(8,128)(2,1)}, u32[]{:S(2)}) copy-start(bf16[1,160,640]{2,1,0:T(8,128)(2,1)} %param.12) | copy-start | bytes 614404
  252.9 102.8 %reduce-scatter.5.cloned.1.call-start = ((), (), s32[]{:S(2)}) async-start(), calls=%async_computation.10 | async-start | bytes 1024000 | tf_op jit(solution)/shard_map/reduce_scatter | solution.py:24
  356.8 16.0 %copy-start.8 = (bf16[160,640]{1,0:T(8,128)(2,1)S(1)}, bf16[160,640]{1,0:T(8,128)(2,1)}, u32[]{:S(2)}) copy-start(bf16[160,640]{1,0:T(8,128)(2,1)} %reduce-scatter.5.cloned.1.call-done) | copy-start | bytes 614404
  369.3 10.9 %all-to-all-start.3 = ((bf16[2,160,640]{2,1,0:T(8,128)(2,1)}), bf16[2,160,640]{2,1,0:T(8,128)(2,1)S(1)}, u32[]{:S(2)}, u32[]{:S(2)}) async-start(bf16[2,160,640]{2,1,0:T(8,128)(2,1)} %broadcast_in_dim.81), calls=%async_computation.5 | async-start | bytes 819200 | tf_op jit(solution)/shard_map/all_to_all | solution.py:30
Sparse Core Ops, SparseCore 0:
  30.8 65.4 all-gather.2
  99.5 115.6 all-gather.4
  253.1 74.6 reduce-scatter.2
  330.2 25.5 reduce-scatter.4
where the time goes:
time: 388 us
  waiting for transfers between devices  284 us (73%)
  matrix products  29.1 us (8%)
  starting transfers between devices  21.8 us (6%)
  local copies, waits for them, and re-layouts  14.4 us (4%)
  between operations  14.2 us (4%)
  other arithmetic  12.4 us (3%)
  blocking collectives  11.7 us (3%)
    all_gather x1, waiting for transfers between devices, side_by_side(): out = lax.all_gather(both, axis, axis=dim, tiled=True)  119 us
    reduce_scatter x2, waiting for transfers between devices, own_rows(): subtotal = lax.psum_scatter(subtotal, axis, scatter_dimension=0, tiled=True)  103 us
    all_gather x1, waiting for transfers between devices, on_device(): clip_rows = lax.all_gather(modulated, 'head', axis=0, tiled=True)  21.1 us
    dot_general x2, matrix products, contract(): return jnp.dot(clip_rows, portion, preferred_element_type=jnp.float32)  14.4 us
    all_to_all x1, waiting for transfers between devices, on_device(): lax.all_to_all(values, 'head', split_axis=1, concat_axis=0, tiled=True)  14.3 us
    all_to_all x1, waiting for transfers between devices, on_device(): lax.all_to_all(cotangent[0], 'head', split_axis=1, concat_axis=0, tiled=T...  13.9 us
    all_to_all x1, blocking collectives, copy_for_each(): lax.all_to_all(jnp.broadcast_to(array[None], (size, *array.shape)), axis,...  11.7 us
    all_to_all x1, starting transfers between devices, on_device(): lax.all_to_all(local_shift.astype(jnp.bfloat16), SEQ, split_axis=0, conca...  11.2 us
  transfers between devices with their start and end apart: 8, of which 8 were waited for; matrix products, arithmetic and copies ran while one was open for 3% of the time, Pallas kernels for 0%

commit v1 on v0

--- a/solution.py
+++ b/solution.py
@@ -4,6 +4,7 @@
 from jax import lax
 from jax.sharding import Mesh
 from jax.sharding import PartitionSpec as P
+from jax.lax import all_to_all, axis_size
 
 HEAD_SIZE = 128
 SEQ = ("seq_0", "seq_1")
@@ -154,7 +155,10 @@
     modulated = (normed * (1.0 + own_shift[0, 1][None, :]) + own_shift[0, 0][None, :]).astype(
         jnp.bfloat16
     )
-    clip_rows = lax.all_gather(modulated, "head", axis=0, tiled=True)
+    fresh = tuple((modulated for _ in range(axis_size("head"))))
+    lower = jnp.stack(fresh, axis=0)
+    response = all_to_all(lower, "head", split_axis=0, concat_axis=0)
+    clip_rows = jnp.concatenate(response, axis=0)
     cosine, sine_table = rope_tables(lattice, HEAD_SIZE)
     own_query = query_weight[0]
 

time: 388 us -> 339 us (0.87)
  waiting for transfers between devices: 284 us -> 195 us
  local copies, waits for them, and re-layouts: 14.4 us -> 46.2 us
  starting transfers between devices: 21.8 us -> 27.7 us
    all_gather x1, waiting for transfers between devices: 119 us -> 59.9 us  [side_by_side(): out = lax.all_gather(both, axis, axis=dim, tiled=True)]
    dot_general x0 -> x3, local copies, waits for them, and re-layouts: none -> 29.6 us  [contract(): return jnp.dot(clip_rows, portion, preferred_element_type=jnp.float32)]
    all_gather x1 -> x0, waiting for transfers between devices: 21.1 us -> none  [on_device(): clip_rows = lax.all_gather(modulated, 'head', axis=0, tiled=True)]
    all_to_all x0 -> x1, starting transfers between devices: none -> 5.21 us  [on_device(): response = all_to_all(lower, 'head', split_axis=0, concat_axis=0)]
    all_to_all x1, waiting for transfers between devices: 14.3 us -> 9.98 us  [on_device(): lax.all_to_all(values, 'head', split_axis=1, concat_axis=0, tiled=True)]
    all_to_all x1, waiting for transfers between devices: 13.9 us -> 9.7 us  [on_device(): lax.all_to_all(cotangent[0], 'head', split_axis=1, concat_axis=0, tiled=T...]
    unnamed x38 -> x34, local copies, waits for them, and re-layouts: 7.86 us -> 4.88 us
  transfers between devices with their start and end apart: 8 -> 8, of which waited for: 8 -> 7; matrix products, arithmetic and copies ran while one was open for 3% -> 11% of each run, Pallas kernels for 0% -> 0%
where the time goes in v1:
time: 339 us; the launch traced here: 338 us
  waiting for transfers between devices  195 us (58%)
  local copies, waits for them, and re-layouts  46.2 us (14%)
  matrix products  32.7 us (10%)
  starting transfers between devices  27.7 us (8%)
  between operations  14.1 us (4%)
  blocking collectives  11.5 us (3%)
  other arithmetic  10.7 us (3%)
    reduce_scatter x2, waiting for transfers between devices, own_rows(): subtotal = lax.psum_scatter(subtotal, axis, scatter_dimension=0, tiled=True)  103 us
    all_gather x1, waiting for transfers between devices, side_by_side(): out = lax.all_gather(both, axis, axis=dim, tiled=True)  59.9 us
    dot_general x3, local copies, waits for them, and re-layouts, contract(): return jnp.dot(clip_rows, portion, preferred_element_type=jnp.float32)  29.6 us
    dot_general x2, matrix products, contract(): return jnp.dot(clip_rows, portion, preferred_element_type=jnp.float32)  14.8 us
    all_to_all x1, blocking collectives, copy_for_each(): lax.all_to_all(jnp.broadcast_to(array[None], (size, *array.shape)), axis,...  11.5 us
    all_to_all x1, starting transfers between devices, on_device(): lax.all_to_all(local_shift.astype(jnp.bfloat16), SEQ, split_axis=0, conca...  11.2 us
    all_to_all x1, waiting for transfers between devices, on_device(): lax.all_to_all(values, 'head', split_axis=1, concat_axis=0, tiled=True)  9.98 us
    all_to_all x1, waiting for transfers between devices, on_device(): lax.all_to_all(cotangent[0], 'head', split_axis=1, concat_axis=0, tiled=T...  9.7 us
  transfers between devices with their start and end apart: 8, of which 7 were waited for; matrix products, arithmetic and copies ran while one was open for 11% of the time, Pallas kernels for 0%

profile of v1, /device:TPU:32, one launch (start us, length us, event | category | flops | bytes accessed | tf_op | source)
XLA Modules:
  0.0 337.8 jit_solution(9999758674598535150)
XLA Ops:
  7.2 0.0 all-gather.2.cloned.1.call-start
  7.2 1.9 pad_maximum_fusion
  9.2 0.0 all-gather.2.cloned.1.call-update
  9.2 0.7 convert_element_type.123
  9.8 0.1 fusion.38
  10.0 0.1 convolution_convert_fusion
  10.2 0.7 copy.51
  10.8 11.2 %all-to-all-start = ((bf16[32,2,160]{2,1,0:T(2,128)(2,1)}), bf16[32,2,160]{2,1,0:T(2,128)(2,1)S(1)}, u32[]{:S(2)}, u32[]{:S(2)}) async-start(bf16[32,2,160]{2,1,0:T(2,128)(2,1)} %copy.51), calls=%async_computation | async-start | bytes 65536 | tf_op jit(solution)/shard_map/all_to_all | solution.py:147
  22.0 0.3 convert_reduce_fusion
  22.3 0.5 fusion.4
  22.8 0.3 copy-done.11
  23.1 1.1 copy.59
  24.2 1.1 copy.57
  25.3 5.5 %all-to-all-done = bf16[32,2,160]{2,1,0:T(2,128)(2,1)S(1)} async-done(((bf16[32,2,160]{2,1,0:T(2,128)(2,1)}), bf16[32,2,160]{2,1,0:T(2,128)(2,1)S(1)}, u32[]{:S(2)}, u32[]{:S(2)}) %all-to-all-start) | async-done | bytes 20512 | tf_op jit(solution)/shard_map/all_to_all | solution.py:147
  30.8 3.5 %all-to-all-start.3 = ((bf16[128,4,640]{0,2,1:T(8,128)(2,1)}), bf16[128,4,640]{0,2,1:T(8,128)(2,1)S(1)}, u32[]{:S(2)}, u32[]{:S(2)}) async-start(bf16[128,4,640]{0,2,1:T(8,128)(2,1)} %bitcast.18), calls=%async_computation.3 | async-start | bytes 1310720 | tf_op jit(solution)/shard_map/all_to_all | solution.py:172
  34.3 0.1 reshape.308
  34.5 10.0 %all-to-all-done.3 = bf16[128,4,640]{0,2,1:T(8,128)(2,1)S(1)} async-done(((bf16[128,4,640]{0,2,1:T(8,128)(2,1)}), bf16[128,4,640]{0,2,1:T(8,128)(2,1)S(1)}, u32[]{:S(2)}, u32[]{:S(2)}) %all-to-all-start.3) | async-done | bytes 655392 | tf_op jit(solution)/shard_map/all_to_all | solution.py:172
  44.5 4.2 %all-to-all-start.2 = ((bf16[128,4,640]{0,2,1:T(8,128)(2,1)}), bf16[128,4,640]{0,2,1:T(8,128)(2,1)}, u32[]{:S(2)}, u32[]{:S(2)}) async-start(bf16[128,4,640]{0,2,1:T(8,128)(2,1)} %bitcast.16), calls=%async_computation.2 | async-start | bytes 1310720 | tf_op jit(solution)/shard_map/all_to_all | solution.py:173
  48.6 0.6 fusion.7
  49.2 9.7 %all-to-all-done.2 = bf16[128,4,640]{0,2,1:T(8,128)(2,1)} async-done(((bf16[128,4,640]{0,2,1:T(8,128)(2,1)}), bf16[128,4,640]{0,2,1:T(8,128)(2,1)}, u32[]{:S(2)}, u32[]{:S(2)}) %all-to-all-start.2) | async-done | bytes 655392 | tf_op jit(solution)/shard_map/all_to_all | solution.py:173
  58.9 3.0 stack.2
  61.9 5.2 %all-to-all-start.1 = ((bf16[4,128,5120]{2,1,0:T(8,128)(2,1)}), bf16[4,128,5120]{2,1,0:T(8,128)(2,1)}, u32[]{:S(2)}, u32[]{:S(2)}) async-start(bf16[4,128,5120]{2,1,0:T(8,128)(2,1)} %stack.2), calls=%async_computation.1 | async-start | bytes 10485760 | tf_op jit(solution)/shard_map/all_to_all | solution.py:160
  67.1 0.0 reduce-scatter.3.cloned.1.call-start
  67.3 2.0 broadcast_multiply_fusion.3
  69.3 0.5 copy.60
  69.8 1.1 reshape.307
  70.9 1.6 copy.58
  72.5 1.1 squeeze.12
  73.6 59.9 %all-gather.2.cloned.1.call-done = bf16[5120,1280]{1,0:T(8,128)(2,1)} async-done(((bf16[160,1280]{1,0:T(8,128)(2,1)}), bf16[5120,1280]{1,0:T(8,128)(2,1)}) %all-gather.2.cloned.1.call-update) | async-done | bytes 13107216 | tf_op jit(solution)/shard_map/all_gather | solution.py:18
  133.5 10.6 %slice_bitcast_fusion = (bf16[640,5120]{0,1:T(8,128)(2,1)}, bf16[640,5120]{0,1:T(8,128)(2,1)}) fusion(bf16[5120,1280]{1,0:T(8,128)(2,1)} %all-gather.2.cloned.1.call-done), kind=kLoop, calls=%fused_computation.1 | loop fusion | bytes 26214400 | tf_op jit(solution)/shard_map/dot_general | solution.py:166
  144.1 9.5 %copy.54 = bf16[640,5120]{1,0:T(8,128)(2,1)} copy(bf16[640,5120]{0,1:T(8,128)(2,1)} %get-tuple-element.14) | data formatting | bytes 13107200 | tf_op jit(solution)/shard_map/dot_general | solution.py:166
  153.6 7.3 %multiply_reduce_fusion.1 = (f32[512,5]{0,1:T(8,128)S(1)}, f32[512,5,128]{0,2,1:T(8,128)S(1)}) fusion(bf16[512,5120,1]{1,0,2:T(8,128)(2,1)} %bitcast.6, bf16[5,128,5120]{2,1,0:T(8,128)(2,1)} %bitcast.58), kind=kOutput, calls=%fused_computation.32 | convolution fusion | flops 3356096000 | bytes 13117440 | tf_op jit(solution)/shard_map/dot_general | solution.py:166
  161.0 0.1 broadcast_multiply_fusion.1
  161.1 1.2 fusion.51
  162.4 9.5 %copy.53 = bf16[640,5120]{1,0:T(8,128)(2,1)} copy(bf16[640,5120]{0,1:T(8,128)(2,1)} %get-tuple-element.15) | data formatting | bytes 13107200 | tf_op jit(solution)/shard_map/dot_general | solution.py:166
  171.9 7.5 %multiply_reduce_fusion.2 = (f32[512,5]{0,1:T(8,128)S(1)}, f32[512,5,128]{0,2,1:T(8,128)S(1)}) fusion(bf16[512,5120,1]{1,0,2:T(8,128)(2,1)} %bitcast.6, bf16[5,128,5120]{2,1,0:T(8,128)(2,1)} %bitcast.59), kind=kOutput, calls=%fused_computation.33 | convolution fusion | flops 3356096000 | bytes 13117440 | tf_op jit(solution)/shard_map/dot_general | solution.py:166
  179.4 0.1 broadcast_multiply_fusion.2
  179.6 0.1 fusion.50
  179.7 0.9 copy-done.4
  180.6 0.2 copy-done.5
  180.8 0.1 copy-done.7
  180.9 0.1 copy-done.8
  181.0 0.4 fusion.24
  181.4 1.1 fusion.1
  182.6 0.1 copy-done.14
  182.7 1.2 fusion.27
  183.9 1.0 copy-done.3
  184.8 5.9 %broadcast_multiply_fusion = (f32[512,5,128]{0,2,1:T(8,128)}, f32[512,5,128]{0,2,1:T(8,128)S(1)}) fusion(f32[512,128]{0,1:T(8,128)} %get-tuple-element.32, bf16[512,5,128]{0,2,1:T(8,128)(2,1)S(1)} %fusion.24, bf16[512,5,128]{0,2,1:T(8,128)(2,1)} %squeeze.12, bf16[512,5,128]{0,2,1:T(8,128)(2,1)} %reshape.307, f32[5,512]{1,0:T(8,128)S(1)} %bitcast.68, ...), kind=kOutput, calls=%fused_computation.39 | convolution fusion | flops 677969920 | bytes 10113024 | tf_op jit(solution)/shard_map/while/body/eval_jaxpr/hqk,khd->qhd/dot_general | solution.py:121
  190.8 1.5 fusion.49
  192.2 0.5 multiply_reduce_fusion
  192.8 0.6 multiply_convert_fusion.5
  193.4 9.5 %multiply_convert_fusion = bf16[5120,640]{1,0:T(8,128)(2,1)} fusion(bf16[512,5120]{1,0:T(8,128)(2,1)} %bitcast.5, bf16[512,640]{0,1:T(8,128)(2,1)S(1)} %bitcast.62), kind=kOutput, calls=%fused_computation | convolution fusion | flops 3361996800 | bytes 12451840 | tf_op jit(solution)/shard_map/dot_general | solution.py:178
  202.9 0.0 reduce-scatter.5.cloned.1.call-start
  203.0 74.8 %reduce-scatter.3.cloned.1.call-done = bf16[640,640]{1,0:T(8,128)(2,1)} async-done(((bf16[5120,640]{1,0:T(8,128)(2,1)}), bf16[640,640]{1,0:T(8,128)(2,1)}) %reduce-scatter.3.cloned.1.call-update) | async-done | bytes 819216 | tf_op jit(solution)/shard_map/reduce_scatter | solution.py:25
  277.8 28.3 %reduce-scatter.5.cloned.1.call-done = bf16[160,640]{1,0:T(8,128)(2,1)} async-done(((bf16[640,640]{1,0:T(8,128)(2,1)}), bf16[160,640]{1,0:T(8,128)(2,1)}) %reduce-scatter.5.cloned.1.call-update) | async-done | bytes 204816 | tf_op jit(solution)/shard_map/reduce_scatter | solution.py:25
  306.1 1.0 fusion.34
  307.2 11.5 %all_to_all.56 = bf16[2,160,640]{2,1,0:T(8,128)(2,1)S(1)} all-to-all(bf16[2,160,640]{2,1,0:T(8,128)(2,1)S(1)} %broadcast_in_dim.82), channel_id=1, replica_groups=mesh['member'=2,'seq_0'=8,'seq_1'=4,'head'=4] {'member'}, dimensions={0} | all-to-all | bytes 819200 | tf_op jit(solution)/shard_map/all_to_all | solution.py:31
  318.7 0.8 broadcast_in_dim.81
  319.5 3.5 %all-to-all-start.4 = ((bf16[2,160,640]{2,1,0:T(8,128)(2,1)}), bf16[2,160,640]{2,1,0:T(8,128)(2,1)S(1)}, u32[]{:S(2)}, u32[]{:S(2)}) async-start(bf16[2,160,640]{2,1,0:T(8,128)(2,1)} %broadcast_in_dim.81), calls=%async_computation.6 | async-start | bytes 819200 | tf_op jit(solution)/shard_map/all_to_all | solution.py:31
  323.0 0.8 convert_bitcast_fusion
  323.8 0.1 convert_reduce_fusion.1
  323.8 6.6 %all-to-all-done.4 = bf16[2,160,640]{2,1,0:T(8,128)(2,1)S(1)} async-done(((bf16[2,160,640]{2,1,0:T(8,128)(2,1)}), bf16[2,160,640]{2,1,0:T(8,128)(2,1)S(1)}, u32[]{:S(2)}, u32[]{:S(2)}) %all-to-all-start.4) | async-done | bytes 409632 | tf_op jit(solution)/shard_map/all_to_all | solution.py:31
  330.4 0.1 convert_reduce_fusion.2
  330.5 0.8 div.63
  (42 shorter events, 0.3 us)
Async XLA Ops:
  7.2 2.8 copy-start
  7.2 14.8 %copy-start.2 = (bf16[128,5120]{1,0:T(8,128)(2,1)S(1)}, bf16[128,5120]{1,0:T(8,128)(2,1)}, u32[]{:S(2)}) copy-start(bf16[128,5120]{1,0:T(8,128)(2,1)} %param.8) | copy-start | bytes 3932164
  7.2 126.4 %all-gather.2.cloned.1.call-start = ((), (), s32[]{:S(2)}) async-start(), calls=%async_computation.8 | async-start | bytes 13516800 | tf_op jit(solution)/shard_map/all_gather | solution.py:18
  10.8 19.9 %all-to-all-start = ((bf16[32,2,160]{2,1,0:T(2,128)(2,1)}), bf16[32,2,160]{2,1,0:T(2,128)(2,1)S(1)}, u32[]{:S(2)}, u32[]{:S(2)}) async-start(bf16[32,2,160]{2,1,0:T(2,128)(2,1)} %copy.51), calls=%async_computation | async-start | bytes 65536 | tf_op jit(solution)/shard_map/all_to_all | solution.py:147
  22.0 1.1 copy-start.11
  22.3 1.9 copy-start.12
  30.8 13.7 %all-to-all-start.3 = ((bf16[128,4,640]{0,2,1:T(8,128)(2,1)}), bf16[128,4,640]{0,2,1:T(8,128)(2,1)S(1)}, u32[]{:S(2)}, u32[]{:S(2)}) async-start(bf16[128,4,640]{0,2,1:T(8,128)(2,1)} %bitcast.18), calls=%async_computation.3 | async-start | bytes 1310720 | tf_op jit(solution)/shard_map/all_to_all | solution.py:172
  44.5 14.5 %all-to-all-start.2 = ((bf16[128,4,640]{0,2,1:T(8,128)(2,1)}), bf16[128,4,640]{0,2,1:T(8,128)(2,1)}, u32[]{:S(2)}, u32[]{:S(2)}) async-start(bf16[128,4,640]{0,2,1:T(8,128)(2,1)} %bitcast.16), calls=%async_computation.2 | async-start | bytes 1310720 | tf_op jit(solution)/shard_map/all_to_all | solution.py:173
  61.9 5.3 %copy-start.15 = (s32[3,512]{1,0:T(4,128)S(1)}, s32[3,512]{1,0:T(4,128)}, u32[]{:S(2)}) copy-start(s32[3,512]{1,0:T(4,128)} %param.9) | copy-start | bytes 18436
  61.9 91.7 %all-to-all-start.1 = ((bf16[4,128,5120]{2,1,0:T(8,128)(2,1)}), bf16[4,128,5120]{2,1,0:T(8,128)(2,1)}, u32[]{:S(2)}, u32[]{:S(2)}) async-start(bf16[4,128,5120]{2,1,0:T(8,128)(2,1)} %stack.2), calls=%async_computation.1 | async-start | bytes 10485760 | tf_op jit(solution)/shard_map/all_to_all | solution.py:160
  67.1 210.6 %reduce-scatter.3.cloned.1.call-start = ((), (), s32[]{:S(2)}) async-start(), calls=%async_computation.9 | async-start | bytes 7372800 | tf_op jit(solution)/shard_map/reduce_scatter | solution.py:25
  179.6 1.1 copy-start.4
  179.6 1.3 copy-start.5
  179.6 1.3 copy-start.7
  179.6 1.4 copy-start.8
  181.4 1.2 copy-start.13
  181.4 1.3 copy-start.14
  182.5 2.3 copy-start.3
  190.8 1.5 copy-start.6
  202.9 103.2 %copy-start.9 = (bf16[1,160,640]{2,1,0:T(8,128)(2,1)S(1)}, bf16[1,160,640]{2,1,0:T(8,128)(2,1)}, u32[]{:S(2)}) copy-start(bf16[1,160,640]{2,1,0:T(8,128)(2,1)} %param.12) | copy-start | bytes 614404
  202.9 103.2 %reduce-scatter.5.cloned.1.call-start = ((), (), s32[]{:S(2)}) async-start(), calls=%async_computation.10 | async-start | bytes 1024000 | tf_op jit(solution)/shard_map/reduce_scatter | solution.py:25
  307.1 15.8 %copy-start.10 = (bf16[160,640]{1,0:T(8,128)(2,1)S(1)}, bf16[160,640]{1,0:T(8,128)(2,1)}, u32[]{:S(2)}) copy-start(bf16[160,640]{1,0:T(8,128)(2,1)} %reduce-scatter.5.cloned.1.call-done) | copy-start | bytes 614404
  319.5 10.9 %all-to-all-start.4 = ((bf16[2,160,640]{2,1,0:T(8,128)(2,1)}), bf16[2,160,640]{2,1,0:T(8,128)(2,1)S(1)}, u32[]{:S(2)}, u32[]{:S(2)}) async-start(bf16[2,160,640]{2,1,0:T(8,128)(2,1)} %broadcast_in_dim.81), calls=%async_computation.6 | async-start | bytes 819200 | tf_op jit(solution)/shard_map/all_to_all | solution.py:31
  323.0 8.3 %copy-start.1 = (bf16[2,256,160]{1,2,0:T(8,128)(2,1)S(1)}, bf16[2,256,160]{1,2,0:T(8,128)(2,1)}, u32[]{:S(2)}) copy-start(bf16[2,256,160]{1,2,0:T(8,128)(2,1)} %param.11) | copy-start | bytes 491524
Sparse Core Ops, SparseCore 0:
  11.2 122.3 all-gather.1
  203.1 74.6 reduce-scatter.2
  280.3 25.7 reduce-scatter.4
